TPU v7x, 32 devices: a whole 2x2x4 slice. The times are simulated.
32 devices in a mesh: groups: 2 (over y), ep: 4 (over z), tp: 2 (over x), dp: 2 (over core).
Axes of the slice: x: 2, y: 2, z: 4, core: 2. Of those that a mesh axis runs over, the one named last changes fastest.
Arguments:
- tokens: bfloat16 [256, 5120], P(('groups', 'ep', 'tp', 'dp')), parts along dimension 0, may hold values from -6 to 6
- route_weights: float32 [256, 8], P(('groups', 'ep', 'tp', 'dp')), parts along dimension 0, may hold values from 0.1 to 1
- expert_ids: int32 [256, 8], P(('groups', 'ep', 'tp', 'dp')), parts along dimension 0, may hold values from 0 to 31, all different within a row; in each aligned block of 8 rows (0 to 7, 8 to 15, ...) at most 4 rows name the same one
- gate_weight: bfloat16 [32, 5120, 1024], P('ep', None, ('tp', 'dp')), may hold values from -0.078125 to 0.078125
- up_weight: bfloat16 [32, 5120, 1024], P('ep', None, ('tp', 'dp')), may hold values from -0.078125 to 0.078125
- down_weight: bfloat16 [32, 1024, 5120], P('ep', None, ('tp', 'dp')), may hold values from -0.1875 to 0.1875
Outputs:
- combined: bfloat16 [256, 5120], P(('groups', 'ep', 'tp', 'dp')), parts along dimension 0
There are 2 independent parts, one for each index of `groups`. A program takes and returns all parts, laid end to end along the dimension named above; an argument that names none is the same for every part. Nothing has to cross between parts.
Inputs may be any that keep to these rules, and one draw needn't show every extreme that they name: `expert_ids`: each row names 8 different experts. Among the 8 rows of one device no expert is named more than 4 times, and in every draw some device's rows name some expert exactly 4 times.
All inputs are finite; a program needn't handle non-finite values.
Results may differ from a plain program's by a relative error of at most 0.0057.
Values may be sent and summed in bfloat16 or wider, within the bound.
No kernel may reach another device: no remote copies, remote signals or barrier semaphores. Data moves between devices by JAX's collectives and lax.ppermute only.
A program may use at most 128 MiB of HBM per device.

v0:
```python
import jax
import jax.numpy as jnp
from jax import lax
from jax.sharding import PartitionSpec as P

CAP = 4


def route_table(ids, experts, capacity):
    tok_count, top_count = ids.shape
    flat = ids.reshape(-1)
    onehot = (flat[:, None] == jnp.arange(experts, dtype=jnp.int32)[None, :]).astype(jnp.int32)
    slots = jnp.sum(onehot * jnp.cumsum(onehot, axis=0), axis=1) - 1
    place = flat * capacity + slots
    owner = jnp.arange(tok_count * top_count, dtype=jnp.int32) // top_count
    table = jnp.full((experts * capacity,), tok_count, jnp.int32).at[place].set(owner)
    return (place, table)


def per_device(tokens, route_weights, expert_ids, gate_weight, up_weight, down_weight):
    n_owner = lax.axis_size("ep")
    tok_count, top_count = expert_ids.shape
    exp_local = gate_weight.shape[0]
    experts = exp_local * n_owner
    width = tokens.shape[1]
    place, table = route_table(expert_ids, experts, CAP)
    sendbuf = jnp.take(tokens, table, axis=0, mode="fill", fill_value=0).reshape(
        experts, CAP, width
    )
    arrived = lax.all_to_all(sendbuf, "ep", split_axis=0, concat_axis=0, tiled=True)
    arrived = arrived.reshape(1, n_owner, exp_local, CAP, width)
    piece = lax.all_gather(arrived, ("tp", "dp"), axis=0, tiled=True)
    gate = jnp.einsum("gsecd,edf->gsecf", piece, gate_weight, preferred_element_type=jnp.float32)
    up = jnp.einsum("gsecd,edf->gsecf", piece, up_weight, preferred_element_type=jnp.float32)
    hidden = (jax.nn.silu(gate) * up).astype(jnp.bfloat16)
    partial_out = jnp.einsum(
        "gsecf,efd->gsecd",
        lax.all_gather(hidden, ("tp", "dp"), axis=4, tiled=True),
        down_weight,
        preferred_element_type=jnp.float32,
    )
    expert_out = partial_out.astype(jnp.bfloat16)
    mine = lax.all_to_all(expert_out, ("tp", "dp"), split_axis=0, concat_axis=4, tiled=True)
    mine = mine.reshape(n_owner * exp_local, CAP, width)
    returned = lax.all_to_all(mine, "ep", split_axis=0, concat_axis=0, tiled=True)
    picked = jnp.take(returned.reshape(experts * CAP, width), place, axis=0)
    picked = picked.reshape(tok_count, top_count, width).astype(jnp.float32)
    combined = jnp.sum(picked * route_weights[:, :, None], axis=1)
    return combined.astype(jnp.bfloat16)


def solution(mesh):
    return jax.shard_map(
        per_device,
        mesh=mesh,
        in_specs=(
            P(("groups", "ep", "tp", "dp"), None),
            P(("groups", "ep", "tp", "dp"), None),
            P(("groups", "ep", "tp", "dp"), None),
            P("ep", None, ("tp", "dp")),
            P("ep", None, ("tp", "dp")),
            P("ep", None, ("tp", "dp")),
        ),
        out_specs=P(("groups", "ep", "tp", "dp"), None),
        check_vma=False,
    )
```

profile of v0, /device:TPU:0, one launch (start us, length us, event | category | flops | bytes accessed | tf_op | source)
XLA Modules:
  0.0 212.0 jit_solution(12040743795864728024)
XLA Ops:
  6.5 0.0 copy-start
  6.5 0.0 all-gather.3.cloned.1.call-start
  6.5 0.8 reshape.76
  7.3 0.7 broadcast_multiply_fusion
  8.0 0.1 fusion.24
  8.1 0.1 reduce_window_sum.11
  8.2 0.2 select_reduce_fusion
  8.4 0.1 mul.40
  8.5 0.8 scatter_custom_fusion
  9.3 0.0 copy-done
  9.3 1.3 gather_fusion
  10.6 0.5 gather.13
  11.1 0.1 broadcast_in_dim.32
  11.3 0.7 broadcast_select_fusion
  11.9 37.5 %all_to_all.25 = bf16[32,4,5120]{2,1,0:T(4,128)(2,1)S(1)} all-to-all(bf16[32,4,5120]{2,1,0:T(4,128)(2,1)S(1)} %broadcast_select_fusion), channel_id=1, replica_groups=mesh['groups'=2,'ep'=4,'tp'=2,'dp'=2] {'ep'}, dimensions={0} | all-to-all | bytes 2621440 | tf_op jit(solution)/shard_map/all_to_all | solution.py:30
  49.4 1.7 copy.13
  51.1 0.0 all-gather.3.cloned.1.call-update
  51.1 0.2 all-gather.5.cloned.1.call-start
  51.3 39.5 %all-gather.3.cloned.1.call-done = bf16[4,4,8,4,5120]{4,3,1,0,2:T(4,128)(2,1)} async-done(((bf16[1,4,8,4,5120]{4,3,1,0,2:T(4,128)(2,1)}), bf16[4,4,8,4,5120]{4,3,1,0,2:T(4,128)(2,1)}) %all-gather.3.cloned.1.call-update) | async-done | bytes 5242896 | tf_op jit(solution)/shard_map/all_gather | solution.py:32
  90.8 0.0 copy-start.4
  90.8 13.1 %fusion.12 = f32[4,4,8,4,256]{4,3,1,0,2:T(4,128)S(1)} fusion(bf16[4,4,8,4,5120]{4,3,1,0,2:T(4,128)(2,1)} %all-gather.3.cloned.1.call-done, bf16[8,5120,256]{2,1,0:T(8,128)(2,1)} %param.9), kind=kOutput, calls=%fused_computation.13 | convolution fusion | flops 1342177280 | bytes 26738688 | tf_op jit(solution)/shard_map/gsecd,edf->gsecf/dot_general | solution.py:33
  103.9 0.0 copy-done.4
  103.9 12.2 %fusion.21 = bf16[4,4,8,4,256]{4,3,1,0,2:T(4,128)(2,1)} fusion(bf16[4,4,8,4,5120]{4,3,1,0,2:T(4,128)(2,1)S(1)} %copy-done.4, bf16[8,5120,256]{2,1,0:T(8,128)(2,1)} %param.10, f32[4,4,8,4,256]{4,3,1,0,2:T(4,128)S(1)} %fusion.12), kind=kOutput, calls=%fused_computation.16 | convolution fusion | flops 1342963712 | bytes 27000832 | tf_op jit(solution)/shard_map/gsecd,edf->gsecf/dot_general | solution.py:34
  116.1 0.0 all-gather.5.cloned.1.call-update
  116.1 17.0 %all-gather.5.cloned.1.call-done = bf16[4,4,8,4,1024]{4,3,1,0,2:T(4,128)(2,1)} async-done(((bf16[4,4,8,4,256]{4,3,1,0,2:T(4,128)(2,1)}), bf16[4,4,8,4,1024]{4,3,1,0,2:T(4,128)(2,1)}) %all-gather.5.cloned.1.call-update) | async-done | bytes 1048592 | tf_op jit(solution)/shard_map/all_gather | solution.py:38
  133.1 11.3 %fusion.9 = bf16[4,4,8,4,1280]{4,3,1,0,2:T(4,128)(2,1)S(1)} fusion(bf16[4,4,8,4,1024]{4,3,1,0,2:T(4,128)(2,1)} %all-gather.5.cloned.1.call-done, bf16[8,1024,1280]{2,1,0:T(8,128)(2,1)} %param.11), kind=kOutput, calls=%fused_computation.10 | convolution fusion | flops 1342832640 | bytes 23330816 | tf_op jit(solution)/shard_map/gsecf,efd->gsecd/dot_general | solution.py:36
  144.4 0.5 copy.14
  144.9 19.7 %all_to_all.26 = bf16[4,4,8,4,1280]{4,3,1,2,0:T(4,128)(2,1)S(1)} all-to-all(bf16[4,4,8,4,1280]{4,3,1,2,0:T(4,128)(2,1)S(1)} %copy.14), channel_id=1, replica_groups=mesh['groups'=2,'ep'=4,'tp'=2,'dp'=2] {'tp','dp'}, dimensions={0} | all-to-all | bytes 2621440 | tf_op jit(solution)/shard_map/all_to_all | solution.py:43
  164.6 1.0 copy.22
  165.6 1.4 reshape.108
  167.0 0.0 copy-start.2
  167.0 4.7 %all-to-all-start.2 = ((bf16[32,4,5120]{2,1,0:T(4,128)(2,1)}), bf16[32,4,5120]{2,1,0:T(4,128)(2,1)S(1)}, u32[]{:S(2)}, u32[]{:S(2)}) async-start(bf16[32,4,5120]{2,1,0:T(4,128)(2,1)} %reshape.108), calls=%async_computation.2 | async-start | bytes 2621440 | tf_op jit(solution)/shard_map/all_to_all | solution.py:45
  171.7 0.1 sub.15
  171.8 0.0 copy-done.2
  171.8 30.9 %all-to-all-done.2 = bf16[32,4,5120]{2,1,0:T(4,128)(2,1)S(1)} async-done(((bf16[32,4,5120]{2,1,0:T(4,128)(2,1)}), bf16[32,4,5120]{2,1,0:T(4,128)(2,1)S(1)}, u32[]{:S(2)}, u32[]{:S(2)}) %all-to-all-start.2) | async-done | bytes 1310752 | tf_op jit(solution)/shard_map/all_to_all | solution.py:45
  202.7 0.3 reshape.79
  203.0 0.0 copy-start.3
  203.0 0.0 copy-start.1
  203.0 0.9 gather_fusion.1
  204.0 0.0 copy-done.3
  204.0 1.2 multiply_reduce_fusion
  205.1 0.0 copy-done.1
  (8 shorter events, 0.0 us)
Async XLA Ops:
  6.5 2.8 %copy-start = (bf16[8,5120]{1,0:T(8,128)(2,1)S(1)}, bf16[8,5120]{1,0:T(8,128)(2,1)}, u32[]{:S(2)}) copy-start(bf16[8,5120]{1,0:T(8,128)(2,1)} %param.6) | copy-start | bytes 245764
  6.5 84.3 %all-gather.3.cloned.1.call-start = ((), (), s32[]{:S(2)}) async-start(), calls=%async_computation.3 | async-start | bytes 6553600 | tf_op jit(solution)/shard_map/all_gather | solution.py:32
  51.1 82.0 %all-gather.5.cloned.1.call-start = ((), (), s32[]{:S(2)}) async-start(), calls=%async_computation.4 | async-start | bytes 1310720 | tf_op jit(solution)/shard_map/all_gather | solution.py:38
  90.8 13.1 %copy-start.4 = (bf16[4,4,8,4,5120]{4,3,1,0,2:T(4,128)(2,1)S(1)}, bf16[4,4,8,4,5120]{4,3,1,0,2:T(4,128)(2,1)}, u32[]{:S(2)}) copy-start(bf16[4,4,8,4,5120]{4,3,1,0,2:T(4,128)(2,1)} %all-gather.3.cloned.1.call-done) | copy-start | bytes 15728644
  167.0 4.8 %copy-start.2 = (s32[8,8]{1,0:T(8,128)S(1)}, s32[8,8]{1,0:T(8,128)}, u32[]{:S(2)}) copy-start(s32[8,8]{1,0:T(8,128)} %param.8) | copy-start | bytes 772
  167.0 35.7 %all-to-all-start.2 = ((bf16[32,4,5120]{2,1,0:T(4,128)(2,1)}), bf16[32,4,5120]{2,1,0:T(4,128)(2,1)S(1)}, u32[]{:S(2)}, u32[]{:S(2)}) async-start(bf16[32,4,5120]{2,1,0:T(4,128)(2,1)} %reshape.108), calls=%async_computation.2 | async-start | bytes 2621440 | tf_op jit(solution)/shard_map/all_to_all | solution.py:45
  203.0 1.0 copy-start.3
  203.0 2.1 %copy-start.1 = (bf16[8,5120]{1,0:T(8,128)(2,1)S(1)}, bf16[8,5120]{1,0:T(8,128)(2,1)}, u32[]{:S(2)}) copy-start(bf16[8,5120]{1,0:T(8,128)(2,1)} %param.6) | copy-start | bytes 245764
Sparse Core Ops, SparseCore 0:
  51.2 39.5 all-gather.2
  116.2 16.8 all-gather.4
where the time goes:
time: 212 us
  waiting for transfers between devices  87.3 us (41%)
  blocking collectives  57.2 us (27%)
  matrix products  36.6 us (17%)
  between operations  13.6 us (6%)
  local copies, waits for them, and re-layouts  9.45 us (4%)
  starting transfers between devices  4.95 us (2%)
  other arithmetic  2.91 us (1%)
    all_gather x1, waiting for transfers between devices, per_device(): piece = lax.all_gather(arrived, ('tp', 'dp'), axis=0, tiled=True)  39.5 us
    all_to_all x1, blocking collectives, per_device(): lax.all_to_all(sendbuf, 'ep', split_axis=0, concat_axis=0, tiled=True)  37.5 us
    all_to_all x1, waiting for transfers between devices, per_device(): lax.all_to_all(mine, 'ep', split_axis=0, concat_axis=0, tiled=True)  30.9 us
    all_to_all x1, blocking collectives, per_device(): lax.all_to_all(expert_out, ('tp', 'dp'), split_axis=0, concat_axis=4, til...  19.7 us
    all_gather x1, waiting for transfers between devices, per_device(): lax.all_gather(hidden, ('tp', 'dp'), axis=4, tiled=True)  17 us
    dot_general x1, matrix products, per_device(): jnp.einsum('gsecd,edf->gsecf', piece, gate_weight, preferred_element_type...  13.1 us
    dot_general x1, matrix products, per_device(): jnp.einsum('gsecd,edf->gsecf', piece, up_weight, preferred_element_type=j...  12.2 us
    dot_general x1, matrix products, per_device(): jnp.einsum('gsecf,efd->gsecd', lax.all_gather(hidden, ('tp', 'dp'), axis=...  11.3 us
  transfers between devices with their start and end apart: 3, of which 3 were waited for; matrix products, arithmetic and copies ran while one was open for 0% of the time, Pallas kernels for 0%

commit v1 on v0

--- a/solution.py
+++ b/solution.py
@@ -33,12 +33,31 @@
     gate = jnp.einsum("gsecd,edf->gsecf", piece, gate_weight, preferred_element_type=jnp.float32)
     up = jnp.einsum("gsecd,edf->gsecf", piece, up_weight, preferred_element_type=jnp.float32)
     hidden = (jax.nn.silu(gate) * up).astype(jnp.bfloat16)
+    tmp = lax.axis_index(("tp", "dp"))
+    newest = lax.axis_size(("tp", "dp"))
+    steps_seen = []
+    next_value, side_arr = (newest, tmp)
+    for idx in range(next_value):
+        steps_seen.append((idx, (idx - 1) % next_value))
+    w1 = hidden
+    state_now = hidden.shape[4]
     partial_out = jnp.einsum(
         "gsecf,efd->gsecd",
-        lax.all_gather(hidden, ("tp", "dp"), axis=4, tiled=True),
-        down_weight,
+        w1,
+        lax.dynamic_slice_in_dim(down_weight, side_arr * state_now, w1.shape[4], axis=1),
         preferred_element_type=jnp.float32,
     )
+    for p in range(1, next_value):
+        w1 = lax.ppermute(w1, ("tp", "dp"), steps_seen)
+        top = jnp.einsum(
+            "gsecf,efd->gsecd",
+            w1,
+            lax.dynamic_slice_in_dim(
+                down_weight, (side_arr + p) % next_value * state_now, w1.shape[4], axis=1
+            ),
+            preferred_element_type=jnp.float32,
+        )
+        partial_out = partial_out + top
     expert_out = partial_out.astype(jnp.bfloat16)
     mine = lax.all_to_all(expert_out, ("tp", "dp"), split_axis=0, concat_axis=4, tiled=True)
     mine = mine.reshape(n_owner * exp_local, CAP, width)

time: 212 us -> 204 us (0.962)
  waiting for transfers between devices: 87.3 us -> 70.5 us
  matrix products: 36.6 us -> 43.3 us
    all_gather x1 -> x0, waiting for transfers between devices: 17 us -> none  [per_device(): lax.all_gather(hidden, ('tp', 'dp'), axis=4, tiled=True)]
    dot_general x1 -> x4, matrix products: 11.3 us -> 18.8 us  [per_device(): jnp.einsum('gsecf,efd->gsecd', w1, lax.dynamic_slice_in_dim(down_weight,...]
    ppermute x0 -> x3, starting transfers between devices: none -> 2.27 us  [per_device(): w1 = lax.ppermute(w1, ('tp', 'dp'), steps_seen)]
  transfers between devices with their start and end apart: 3 -> 5, of which waited for: 3 -> 2; matrix products, arithmetic and copies ran while one was open for 0% -> 8% of each run, Pallas kernels for 0% -> 0%
where the time goes in v1:
time: 204 us
  waiting for transfers between devices  70.5 us (35%)
  blocking collectives  57.3 us (28%)
  matrix products  43.3 us (21%)
  between operations  13.6 us (7%)
  local copies, waits for them, and re-layouts  9.42 us (5%)
  starting transfers between devices  6.86 us (3%)
  other arithmetic  2.94 us (1%)
    all_gather x1, waiting for transfers between devices, per_device(): piece = lax.all_gather(arrived, ('tp', 'dp'), axis=0, tiled=True)  39.7 us
    all_to_all x1, blocking collectives, per_device(): lax.all_to_all(sendbuf, 'ep', split_axis=0, concat_axis=0, tiled=True)  37.5 us
    all_to_all x1, waiting for transfers between devices, per_device(): lax.all_to_all(mine, 'ep', split_axis=0, concat_axis=0, tiled=True)  30.9 us
    all_to_all x1, blocking collectives, per_device(): lax.all_to_all(expert_out, ('tp', 'dp'), split_axis=0, concat_axis=4, til...  19.8 us
    dot_general x4, matrix products, per_device(): jnp.einsum('gsecf,efd->gsecd', w1, lax.dynamic_slice_in_dim(down_weight,...  18.8 us
    dot_general x1, matrix products, per_device(): jnp.einsum('gsecd,edf->gsecf', piece, gate_weight, preferred_element_type...  13.1 us
    dot_general x1, matrix products, per_device(): jnp.einsum('gsecd,edf->gsecf', piece, up_weight, preferred_element_type=j...  11.5 us
    all_to_all x1, starting transfers between devices, per_device(): lax.all_to_all(mine, 'ep', split_axis=0, concat_axis=0, tiled=True)  4.59 us
  transfers between devices with their start and end apart: 5, of which 2 were waited for; matrix products, arithmetic and copies ran while one was open for 8% of the time, Pallas kernels for 0%

profile of v1, /device:TPU:0, one launch (start us, length us, event | category | flops | bytes accessed | tf_op | source)
XLA Modules:
  0.0 204.0 jit_solution(1387919113791989825)
XLA Ops:
  6.5 0.0 copy-start
  6.5 0.0 all-gather.2.cloned.1.call-start
  6.5 0.7 broadcast_multiply_fusion
  7.3 0.8 reshape.76
  8.0 0.1 mul.57
  8.1 0.1 fusion.43
  8.2 0.1 reduce_window_sum.11
  8.3 0.2 select_reduce_fusion
  8.5 0.8 scatter_custom_fusion
  9.3 0.0 copy-done
  9.3 1.3 gather_fusion
  10.6 0.5 gather.13
  11.1 0.1 broadcast_in_dim.32
  11.3 0.7 broadcast_select_fusion
  11.9 37.5 %all_to_all.25 = bf16[32,4,5120]{2,1,0:T(4,128)(2,1)S(1)} all-to-all(bf16[32,4,5120]{2,1,0:T(4,128)(2,1)S(1)} %broadcast_select_fusion), channel_id=1, replica_groups=mesh['groups'=2,'ep'=4,'tp'=2,'dp'=2] {'ep'}, dimensions={0} | all-to-all | bytes 2621440 | tf_op jit(solution)/shard_map/all_to_all | solution.py:30
  49.4 1.6 copy.13
  51.0 0.0 all-gather.2.cloned.1.call-update
  51.1 39.7 %all-gather.2.cloned.1.call-done = bf16[4,4,8,4,5120]{4,3,1,0,2:T(4,128)(2,1)} async-done(((bf16[1,4,8,4,5120]{4,3,1,0,2:T(4,128)(2,1)}), bf16[4,4,8,4,5120]{4,3,1,0,2:T(4,128)(2,1)}) %all-gather.2.cloned.1.call-update) | async-done | bytes 5242896 | tf_op jit(solution)/shard_map/all_gather | solution.py:32
  90.8 13.1 %fusion.31 = f32[4,4,8,4,256]{4,3,1,0,2:T(4,128)S(1)} fusion(bf16[4,4,8,4,5120]{4,3,1,0,2:T(4,128)(2,1)} %all-gather.2.cloned.1.call-done, bf16[8,5120,256]{2,1,0:T(8,128)(2,1)} %param.9), kind=kOutput, calls=%fused_computation.26 | convolution fusion | flops 1342177280 | bytes 26738688 | tf_op jit(solution)/shard_map/gsecd,edf->gsecf/dot_general | solution.py:33
  103.9 0.0 copy-done.4
  103.9 11.5 %fusion.40 = bf16[4,4,8,4,256]{4,3,1,0,2:T(4,128)(2,1)S(1)} fusion(bf16[4,4,8,4,5120]{4,3,1,0,2:T(4,128)(2,1)S(1)} %copy-done.4, bf16[8,5120,256]{2,1,0:T(8,128)(2,1)} %param.10, f32[4,4,8,4,256]{4,3,1,0,2:T(4,128)S(1)} %fusion.31), kind=kOutput, calls=%fused_computation.29 | convolution fusion | flops 1342963712 | bytes 27000832 | tf_op jit(solution)/shard_map/gsecd,edf->gsecf/dot_general | solution.py:34
  115.4 0.2 collective-permute-start
  115.6 5.0 %fusion.10 = f32[8,1280,4,4,4]{1,4,3,2,0:T(4,128)} fusion(bf16[4,4,8,4,256]{4,3,1,0,2:T(4,128)(2,1)S(1)} %fusion.40, bf16[8,1024,1280]{2,1,0:T(8,128)(2,1)} %param.11, s32[]{:T(128)S(6)} %select_n.65), kind=kOutput, calls=%fused_computation.13 | convolution fusion | flops 335544320 | bytes 8126468 | tf_op jit(solution)/shard_map/gsecf,efd->gsecd/dot_general | solution.py:44
  120.6 0.0 collective-permute-done
  120.6 0.8 collective-permute-start.1
  121.4 6.7 %fusion.16 = f32[8,1280,4,4,4]{1,4,3,2,0:T(4,128)} fusion(f32[8,1280,4,4,4]{1,4,3,2,0:T(4,128)} %fusion.10, bf16[4,4,8,4,256]{4,3,1,0,2:T(4,128)(2,1)S(1)} %collective-permute-done, bf16[8,1024,1280]{2,1,0:T(8,128)(2,1)} %param.11, s32[]{:T(128)S(6)} %select_n.71), kind=kOutput, calls=%fused_computation.19 | convolution fusion | flops 336199680 | bytes 10747908 | tf_op jit(solution)/shard_map/gsecf,efd->gsecd/dot_general | solution.py:52
  128.1 0.0 collective-permute-done.1
  128.1 1.3 collective-permute-start.2
  129.3 0.0 slice-done
  129.3 0.0 slice-done.1
  129.3 0.0 slice-done.2
  129.3 0.0 slice-done.3
  129.3 0.0 slice-done.4
  129.4 4.3 %fusion.19 = f32[8,1280,4,4,4]{1,4,3,2,0:T(4,128)} fusion(f32[8,1280,4,4,4]{1,4,3,2,0:T(4,128)} %fusion.16, bf16[4,4,8,4,256]{4,3,1,0,2:T(4,128)(2,1)S(1)} %collective-permute-done.1, bf16[8,1024,1280]{2,1,0:T(8,128)(2,1)S(1)} %bitcast.81, s32[]{:T(128)S(6)} %select_n.73), kind=kOutput, calls=%fused_computation.20 | convolution fusion | flops 336199680 | bytes 10747908 | tf_op jit(solution)/shard_map/gsecf,efd->gsecd/dot_general | solution.py:52
  133.7 0.0 collective-permute-done.2
  133.7 2.8 %fusion.28 = bf16[4,4,8,4,1280]{4,3,1,0,2:T(4,128)(2,1)S(1)} fusion(f32[8,1280,4,4,4]{1,4,3,2,0:T(4,128)} %fusion.19, bf16[4,4,8,4,256]{4,3,1,0,2:T(4,128)(2,1)S(1)} %collective-permute-done.2, bf16[8,1024,1280]{2,1,0:T(8,128)(2,1)S(1)} %bitcast.81, s32[]{:T(128)S(6)} %select_n.75), kind=kOutput, calls=%fused_computation.23 | convolution fusion | flops 336855040 | bytes 9437188 | tf_op jit(solution)/shard_map/gsecf,efd->gsecd/dot_general | solution.py:52
  136.5 0.5 copy.14
  136.9 19.8 %all_to_all.26 = bf16[4,4,8,4,1280]{4,3,1,2,0:T(4,128)(2,1)S(1)} all-to-all(bf16[4,4,8,4,1280]{4,3,1,2,0:T(4,128)(2,1)S(1)} %copy.14), channel_id=1, replica_groups=mesh['groups'=2,'ep'=4,'tp'=2,'dp'=2] {'tp','dp'}, dimensions={0} | all-to-all | bytes 2621440 | tf_op jit(solution)/shard_map/all_to_all | solution.py:62
  156.7 1.0 copy.25
  157.7 0.0 copy-start.2
  157.7 1.4 reshape.111
  159.1 4.6 %all-to-all-start.2 = ((bf16[32,4,5120]{2,1,0:T(4,128)(2,1)}), bf16[32,4,5120]{2,1,0:T(4,128)(2,1)S(1)}, u32[]{:S(2)}, u32[]{:S(2)}) async-start(bf16[32,4,5120]{2,1,0:T(4,128)(2,1)} %reshape.111), calls=%async_computation.2 | async-start | bytes 2621440 | tf_op jit(solution)/shard_map/all_to_all | solution.py:64
  163.7 0.1 sub.15
  163.8 30.9 %all-to-all-done.2 = bf16[32,4,5120]{2,1,0:T(4,128)(2,1)S(1)} async-done(((bf16[32,4,5120]{2,1,0:T(4,128)(2,1)}), bf16[32,4,5120]{2,1,0:T(4,128)(2,1)S(1)}, u32[]{:S(2)}, u32[]{:S(2)}) %all-to-all-start.2) | async-done | bytes 1310752 | tf_op jit(solution)/shard_map/all_to_all | solution.py:64
  194.7 0.3 reshape.79
  195.0 0.0 copy-start.3
  195.0 0.9 gather_fusion.1
  196.0 1.2 multiply_reduce_fusion
  (19 shorter events, 0.1 us)
Async XLA Ops:
  6.5 2.8 %copy-start = (bf16[8,5120]{1,0:T(8,128)(2,1)S(1)}, bf16[8,5120]{1,0:T(8,128)(2,1)}, u32[]{:S(2)}) copy-start(bf16[8,5120]{1,0:T(8,128)(2,1)} %param.6) | copy-start | bytes 245764
  6.5 84.2 %all-gather.2.cloned.1.call-start = ((), (), s32[]{:S(2)}) async-start(), calls=%async_computation.3 | async-start | bytes 6553600 | tf_op jit(solution)/shard_map/all_gather | solution.py:32
  90.8 13.1 %copy-start.4 = (bf16[4,4,8,4,5120]{4,3,1,0,2:T(4,128)(2,1)S(1)}, bf16[4,4,8,4,5120]{4,3,1,0,2:T(4,128)(2,1)}, u32[]{:S(2)}) copy-start(bf16[4,4,8,4,5120]{4,3,1,0,2:T(4,128)(2,1)} %all-gather.2.cloned.1.call-done) | copy-start | bytes 15728644
  115.4 5.3 %collective-permute-start = (bf16[4,4,8,4,256]{4,3,1,0,2:T(4,128)(2,1)S(1)}, bf16[4,4,8,4,256]{4,3,1,0,2:T(4,128)(2,1)S(1)}, u32[]{:S(2)}, u32[]{:S(2)}) collective-permute-start(bf16[4,4,8,4,256]{4,3,1,0,2:T(4,128)(2,1)S(1)} %fusion.40), channel_id=1, source_target_pairs={{0,3},{1,0},{2,1},{3,2},{4,7},{5,4},{6,5},{7,6},{8,11},{9,8},{10,9... | collective-permute-start | bytes 786440 | tf_op jit(solution)/shard_map/ppermute | solution.py:51
  115.6 13.7 %slice-start = ((s8[20971520]{0:T(1024)(128)(4,1)}), s8[4194304]{0:T(1024)(128)(4,1)S(1)}, s32[]{:S(2)}) async-start(s8[20971520]{0:T(1024)(128)(4,1)} %bitcast.80), calls=%async_computation.4 | async-start | bytes 8388608
  115.6 13.7 %slice-start.1 = ((s8[20971520]{0:T(1024)(128)(4,1)}), s8[4194304]{0:T(1024)(128)(4,1)S(1)}, s32[]{:S(2)}) async-start(s8[20971520]{0:T(1024)(128)(4,1)} %bitcast.80), calls=%async_computation.5 | async-start | bytes 8388608
  115.6 13.7 %slice-start.2 = ((s8[20971520]{0:T(1024)(128)(4,1)}), s8[4194304]{0:T(1024)(128)(4,1)S(1)}, s32[]{:S(2)}) async-start(s8[20971520]{0:T(1024)(128)(4,1)} %bitcast.80), calls=%async_computation.6 | async-start | bytes 8388608
  120.6 8.7 %slice-start.3 = ((s8[20971520]{0:T(1024)(128)(4,1)}), s8[4194304]{0:T(1024)(128)(4,1)S(1)}, s32[]{:S(2)}) async-start(s8[20971520]{0:T(1024)(128)(4,1)} %bitcast.80), calls=%async_computation.7 | async-start | bytes 8388608
  120.6 8.7 %slice-start.4 = ((s8[20971520]{0:T(1024)(128)(4,1)}), s8[4194304]{0:T(1024)(128)(4,1)S(1)}, s32[]{:S(2)}) async-start(s8[20971520]{0:T(1024)(128)(4,1)} %bitcast.80), calls=%async_computation.8 | async-start | bytes 8388608
  120.6 7.4 %collective-permute-start.1 = (bf16[4,4,8,4,256]{4,3,1,0,2:T(4,128)(2,1)S(1)}, bf16[4,4,8,4,256]{4,3,1,0,2:T(4,128)(2,1)S(1)}, u32[]{:S(2)}, u32[]{:S(2)}) collective-permute-start(bf16[4,4,8,4,256]{4,3,1,0,2:T(4,128)(2,1)S(1)} %collective-permute-done), channel_id=1, source_target_pairs={{0,3},{1,0},{2,1},{3,2},{4,7},{5,4},{6,5},{7,6},{8,11},{9,8},{10,9... | collective-permute-start | bytes 786440 | tf_op jit(solution)/shard_map/ppermute | solution.py:51
  128.1 5.6 %collective-permute-start.2 = (bf16[4,4,8,4,256]{4,3,1,0,2:T(4,128)(2,1)S(1)}, bf16[4,4,8,4,256]{4,3,1,0,2:T(4,128)(2,1)S(1)}, u32[]{:S(2)}, u32[]{:S(2)}) collective-permute-start(bf16[4,4,8,4,256]{4,3,1,0,2:T(4,128)(2,1)S(1)} %collective-permute-done.1), channel_id=1, source_target_pairs={{0,3},{1,0},{2,1},{3,2},{4,7},{5,4},{6,5},{7,6},{8,11},{9,8},{10,9... | collective-permute-start | bytes 786440 | tf_op jit(solution)/shard_map/ppermute | solution.py:51
  157.7 6.1 %copy-start.2 = (s32[8,8]{1,0:T(8,128)S(1)}, s32[8,8]{1,0:T(8,128)}, u32[]{:S(2)}) copy-start(s32[8,8]{1,0:T(8,128)} %param.8) | copy-start | bytes 772
  159.1 35.6 %all-to-all-start.2 = ((bf16[32,4,5120]{2,1,0:T(4,128)(2,1)}), bf16[32,4,5120]{2,1,0:T(4,128)(2,1)S(1)}, u32[]{:S(2)}, u32[]{:S(2)}) async-start(bf16[32,4,5120]{2,1,0:T(4,128)(2,1)} %reshape.111), calls=%async_computation.2 | async-start | bytes 2621440 | tf_op jit(solution)/shard_map/all_to_all | solution.py:64
  194.7 2.5 %copy-start.1 = (bf16[8,5120]{1,0:T(8,128)(2,1)S(1)}, bf16[8,5120]{1,0:T(8,128)(2,1)}, u32[]{:S(2)}) copy-start(bf16[8,5120]{1,0:T(8,128)(2,1)} %param.6) | copy-start | bytes 245764
  195.0 0.9 copy-start.3
Sparse Core Ops, SparseCore 0:
  51.2 39.5 all-gather.1
